TPU v7x, 32 devices: a whole 2x2x4 slice. The times are simulated.
32 devices in a mesh: groups: 2 (over y), gx: 4 (over z), gy: 4 (over x, core).
Axes of the slice: x: 2, y: 2, z: 4, core: 2. Of those that a mesh axis runs over, the one named last changes fastest.
Arguments:
- thermal_deviation: float32 [32, 256, 512], P('groups', 'gy', 'gx'), parts along dimension 0, may hold values from -6 to 6
- brine_content: float32 [32, 256, 512], P('groups', 'gy', 'gx'), parts along dimension 0, may hold values from 0.2 to 2.4
- current_components: float32 [4, 16, 256, 512], P('groups', None, 'gy', 'gx'), parts along dimension 0, may hold values from -4 to 4
- sea_indicator: int32 [256, 512], P('gy', 'gx'), may hold values from 0 to 1, as said below
- flooded_layer_number: int32 [256, 512], P('gy', 'gx'), may hold values from 1 to 16
- footprint_square_metres: float32 [256, 512], P('gy', 'gx'), may hold values from 0.5 to 5
- rainfall_input: float32 [256, 512], P('gy', 'gx'), may hold values from -2 to 3.5
- seam_partner_index: int32 [512], P('gx'), may hold values from 0 to 511, as said below
Outputs:
- temperature_next: float32 [32, 256, 512], P('groups', 'gy', 'gx'), parts along dimension 0
- salinity_next: float32 [32, 256, 512], P('groups', 'gy', 'gx'), parts along dimension 0
There are 2 independent parts, one for each index of `groups`. A program takes and returns all parts, laid end to end along the dimension named above; an argument that names none is the same for every part. Nothing has to cross between parts.
Inputs may be any that keep to these rules, and one draw needn't show every extreme that they name: `sea_indicator`: at least one column is ocean. seam_partner_index[x] = (s - x) mod 512 for one s of each draw with s mod 128 = 127; the map is its own inverse and has no fixed point.
All inputs are finite; a program needn't handle non-finite values.
Results may differ from a plain program's by a relative error of at most 0.00002.
Values sent between devices are 32-bit elements; how exact they have to be, the bound alone decides.
A program may use at most 64 MiB of HBM per device.

v0:
```python
import jax
import jax.numpy as jnp
from jax import lax
from jax.sharding import PartitionSpec as P

time_step = 0.25
diffusivity = 0.5
vertical_mixing = 0.3
top_thickness = 0.5


def with_halo(cells, sides, width, closed):
    for axis, dim in sides:
        count = lax.axis_size(axis)
        ends = count if closed else count - 1
        head = lax.slice_in_dim(cells, 0, width, axis=dim)
        tail = lax.slice_in_dim(cells, cells.shape[dim] - width, cells.shape[dim], axis=dim)
        cells = jnp.concatenate(
            [
                lax.ppermute(tail, axis, [(i, (i + 1) % count) for i in range(ends)]),
                cells,
                lax.ppermute(head, axis, [((i + 1) % count, i) for i in range(ends)]),
            ],
            axis=dim,
        )
    return cells


def face_flux(near_cells, far_cells, face_speed, near_wet, far_wet):
    upwind = jnp.maximum(face_speed, 0.0) * near_cells + jnp.minimum(face_speed, 0.0) * far_cells
    return near_wet * far_wet * (upwind - diffusivity * (far_cells - near_cells))


def wet_from(depth_plane, layer_stack_number):
    level_index = jnp.arange(layer_stack_number, dtype=jnp.float32)
    return (level_index[:, None, None] < depth_plane[None]).astype(jnp.float32)


def split_tracer(block_planes, layer_stack_number):
    return block_planes[: 2 * layer_stack_number].reshape(
        (2, layer_stack_number) + block_planes.shape[1:]
    )


def shards(
    thermal_deviation,
    brine_content,
    current_components,
    sea_indicator,
    flooded_layer_number,
    footprint_square_metres,
    rainfall_input,
    seam_partner_index,
):
    layer_stack_number, parallel_total_number, meridian_total_number = thermal_deviation.shape
    stacked_layer_number = (sea_indicator * flooded_layer_number).astype(jnp.float32)
    wet_area = footprint_square_metres * sea_indicator.astype(jnp.float32)
    surface = brine_content[0]
    total_area, total_fresh, salt_fresh, salt_only = lax.psum(
        (
            jnp.sum(wet_area),
            jnp.sum(wet_area * rainfall_input),
            jnp.sum(wet_area * surface * rainfall_input),
            jnp.sum(wet_area * surface),
        ),
        ("gx", "gy"),
    )
    mean_fresh = total_fresh / total_area
    balanced = rainfall_input - mean_fresh
    total_salt = salt_fresh - mean_fresh * salt_only
    virtual = -surface * balanced + total_salt / total_area
    top_row = jnp.concatenate(
        [
            thermal_deviation[:, -1, :],
            brine_content[:, -1, :],
            current_components[1][:, -1, :],
            stacked_layer_number[-1:, :],
        ],
        axis=0,
    )
    gathered = lax.all_gather(top_row, "gx", axis=1, tiled=True)
    partner_row = jnp.take(gathered, seam_partner_index, axis=1)
    partner_fields = jnp.concatenate(
        [partner_row[: 2 * layer_stack_number], partner_row[3 * layer_stack_number :]], axis=0
    )
    partner_speed = partner_row[2 * layer_stack_number : 3 * layer_stack_number]
    is_top = lax.axis_index("gy") == lax.axis_size("gy") - 1
    planes = jnp.concatenate(
        [
            thermal_deviation,
            brine_content,
            current_components[0],
            current_components[1],
            stacked_layer_number[None],
        ],
        axis=0,
    )
    zonal_padded = with_halo(planes, (("gx", 2),), 1, True)
    meridional_padded = with_halo(planes, (("gy", 1),), 1, False)
    zonal_tracer = split_tracer(zonal_padded, layer_stack_number)
    zonal_wet = wet_from(zonal_padded[4 * layer_stack_number], layer_stack_number)
    zonal_near_speed = zonal_padded[2 * layer_stack_number : 3 * layer_stack_number][..., :-1]
    halo_top = jnp.concatenate(
        [
            meridional_padded[: 2 * layer_stack_number, -1, :],
            meridional_padded[4 * layer_stack_number :, -1, :],
        ],
        axis=0,
    )
    above_fields = jnp.where(is_top, partner_fields, halo_top)
    upper_tracer_cells = jnp.concatenate(
        [
            meridional_padded[: 2 * layer_stack_number, 1:-1, :],
            above_fields[: 2 * layer_stack_number, None, :],
        ],
        axis=1,
    )
    upper_depth = jnp.concatenate(
        [
            meridional_padded[4 * layer_stack_number, 1:-1, :],
            above_fields[2 * layer_stack_number][None, :],
        ],
        axis=0,
    )
    lower_cells = meridional_padded[:, :-1, :]
    lower_tracer = split_tracer(lower_cells, layer_stack_number)
    lower_wet = wet_from(lower_cells[4 * layer_stack_number], layer_stack_number)
    upper_tracer = split_tracer(upper_tracer_cells, layer_stack_number)
    upper_wet = wet_from(upper_depth, layer_stack_number)
    north_speed = lower_cells[3 * layer_stack_number : 4 * layer_stack_number]
    carried_quantity = jnp.stack([thermal_deviation, brine_content])
    wet_cells = wet_from(stacked_layer_number, layer_stack_number)
    zonal_flux = face_flux(
        zonal_tracer[..., :-1],
        zonal_tracer[..., 1:],
        zonal_near_speed,
        zonal_wet[..., :-1],
        zonal_wet[..., 1:],
    )
    fold_speed = 0.5 * (north_speed[:, -1, :] - partner_speed)
    last_speed = jnp.where(is_top, fold_speed, north_speed[:, -1, :])
    north_speed = jnp.concatenate([north_speed[:, :-1, :], last_speed[:, None, :]], axis=1)
    meridional_flux = face_flux(lower_tracer, upper_tracer, north_speed, lower_wet, upper_wet)
    vertical = (
        wet_cells[:-1]
        * wet_cells[1:]
        * vertical_mixing
        * (carried_quantity[:, :-1] - carried_quantity[:, 1:])
    )
    zero_layer = jnp.zeros_like(vertical[:, :1])
    from_above = jnp.concatenate([zero_layer, vertical], axis=1)
    to_below = jnp.concatenate([vertical, zero_layer], axis=1)
    tendency = time_step / footprint_square_metres * (
        zonal_flux[..., :-1]
        - zonal_flux[..., 1:]
        + meridional_flux[:, :, :-1]
        - meridional_flux[:, :, 1:]
    ) + time_step * (from_above - to_below)
    updated = carried_quantity + wet_cells * tendency
    surface_next = updated[1, 0] + time_step / top_thickness * virtual * wet_cells[0]
    salinity_next = jnp.concatenate([surface_next[None], updated[1, 1:]], axis=0)
    return (updated[0], salinity_next)


def solution(mesh):
    in_specs = (
        P("groups", "gy", "gx"),
        P("groups", "gy", "gx"),
        P("groups", None, "gy", "gx"),
        P("gy", "gx"),
        P("gy", "gx"),
        P("gy", "gx"),
        P("gy", "gx"),
        P("gx"),
    )
    out_specs = (P("groups", "gy", "gx"), P("groups", "gy", "gx"))
    return jax.shard_map(shards, mesh=mesh, in_specs=in_specs, out_specs=out_specs, check_vma=False)
```

profile of v0, /device:TPU:0, one launch (start us, length us, event | category | flops | bytes accessed | tf_op | source)
XLA Modules:
  0.0 111.4 jit_solution(16813490816440808588)
XLA Ops:
  0.6 2.3 %constant_dynamic-update-slice_fusion.2 = (f32[65,64,128]{2,0,1:T(8,128)S(1)}, f32[16,64,128]{2,0,1:T(8,128)}) fusion(f32[16,64,128]{2,1,0:T(8,128)} %param.8), kind=kLoop, calls=%fused_computation.82 | loop fusion | bytes 1572864
  3.1 1.1 %constant_dynamic-update-slice_fusion.1 = (f32[65,64,128]{2,0,1:T(8,128)S(1)}, f32[16,64,128]{2,0,1:T(8,128)}) fusion(f32[65,64,128]{2,0,1:T(8,128)S(1)} %get-tuple-element.22, f32[16,64,128]{2,1,0:T(8,128)S(1)} %copy-done.2), kind=kLoop, calls=%fused_computation.81 | loop fusion | bytes 1572864
  5.0 2.9 %fusion.24 = (f32[65,64,1]{2,0,1:T(8,128)}, f32[65,64,1]{2,0,1:T(8,128)}) fusion(f32[65,64,128]{2,0,1:T(8,128)S(1)} %dynamic-update-slice.4), kind=kLoop, calls=%fused_computation.87 | loop fusion | bytes 66560 | tf_op jit(solution)/shard_map/slice | solution.py:17
  7.9 3.1 %copy.160 = f32[65,64,1]{0,1,2:T(8,128)} copy(f32[65,64,1]{2,0,1:T(8,128)} %get-tuple-element.14) | data formatting | bytes 33280 | tf_op jit(solution)/shard_map/slice | solution.py:17
  11.0 3.1 %collective-permute-start = (f32[65,64,1]{0,1,2:T(8,128)}, f32[65,64,1]{0,1,2:T(8,128)}, u32[]{:S(2)}, u32[]{:S(2)}) collective-permute-start(f32[65,64,1]{0,1,2:T(8,128)} %copy.160), channel_id=1, source_target_pairs={{0,4},{4,8},{8,12},{12,0},{1,5},{5,9},{9,13},{13,1},{2,6},{6,10},{... | collective-permute-start | bytes 49928 | tf_op jit(solution)/shard_map/ppermute | solution.py:20
  14.0 3.1 %copy.161 = f32[65,64,1]{0,1,2:T(8,128)} copy(f32[65,64,1]{2,0,1:T(8,128)} %get-tuple-element.15) | data formatting | bytes 33280 | tf_op jit(solution)/shard_map/slice | solution.py:16
  17.1 2.1 %collective-permute-start.1 = (f32[65,64,1]{0,1,2:T(8,128)}, f32[65,64,1]{0,1,2:T(8,128)}, u32[]{:S(2)}, u32[]{:S(2)}) collective-permute-start(f32[65,64,1]{0,1,2:T(8,128)} %copy.161), channel_id=1, source_target_pairs={{4,0},{8,4},{12,8},{0,12},{5,1},{9,5},{13,9},{1,13},{6,2},{10,6},{... | collective-permute-start | bytes 49928 | tf_op jit(solution)/shard_map/ppermute | solution.py:22
  19.8 1.3 %collective-permute-start.2 = (f32[65,1,128]{2,0,1:T(8,128)}, f32[65,1,128]{2,0,1:T(8,128)}, u32[]{:S(2)}, u32[]{:S(2)}) collective-permute-start(f32[65,1,128]{2,0,1:T(8,128)} %get-tuple-element.17), channel_id=1, source_target_pairs={{1,0},{2,1},{3,2},{5,4},{6,5},{7,6},{9,8},{10,9},{11,10},{13,12},{... | collective-permute-start | bytes 99848 | tf_op jit(solution)/shard_map/ppermute | solution.py:22
  21.1 3.6 %collective-permute-start.3 = (f32[65,1,128]{2,0,1:T(8,128)}, f32[65,1,128]{2,0,1:T(8,128)}, u32[]{:S(2)}, u32[]{:S(2)}) collective-permute-start(f32[65,1,128]{2,0,1:T(8,128)} %get-tuple-element.16), channel_id=1, source_target_pairs={{0,1},{1,2},{2,3},{4,5},{5,6},{6,7},{8,9},{9,10},{10,11},{12,13},{... | collective-permute-start | bytes 99848 | tf_op jit(solution)/shard_map/ppermute | solution.py:20
  24.7 1.3 %copy.203 = f32[1,16,64,128]{3,1,2,0:T(8,128)S(1)} copy(f32[1,16,64,128]{3,2,1,0:T(8,128)} %copy-done.5) | data formatting | bytes 1048576
  27.3 1.1 pad_maximum_fusion.6
  30.6 13.3 %all_gather.3 = f32[49,512]{1,0:T(8,128)S(1)} all-gather(f32[49,128]{1,0:T(8,128)S(1)} %pad_maximum_fusion.11), channel_id=1, replica_groups=mesh['groups'=2,'gx'=4,'gy'=4] {'gx'}, dimensions={1}, use_global_device_ids=true | all-gather | bytes 125440 | tf_op jit(solution)/shard_map/all_gather | solution.py:81
  45.4 1.6 %gather_fusion = f32[128,49]{1,0:T(8,128)S(1)} fusion(f32[49,512]{0,1:T(8,128)} %copy.172, s32[1024]{0:T(1024)S(1)} %pad_clamp_fusion), kind=kCustom, calls=%fused_computation | custom fusion | bytes 50688 | tf_op jit(solution)/shard_map/jit(_take)/gather | solution.py:82
  47.7 2.0 %fusion.12 = f32[15,64,128]{2,1,0:T(8,128)} fusion(f32[16,64,128]{2,1,0:T(8,128)} %fusion.11), kind=kLoop, calls=%fused_computation.45 | loop fusion | flops 245760 | bytes 1474560 | tf_op jit(solution)/shard_map/mul | solution.py:145
  50.6 1.4 %select_bitcast_fusion = f32[49,128]{1,0:T(8,128)} fusion(f32[128,49]{0,1:T(8,128)} %copy.173, pred[128]{0:T(512)(128)(4,1)} %compare_and_fusion), kind=kLoop, calls=%fused_computation.68 | loop fusion | flops 6272 | bytes 50304 | tf_op jit(solution)/shard_map/jit(_take)/select_n | solution.py:82
  52.6 2.1 %fusion.7 = f32[2,15,64,128]{3,2,1,0:T(8,128)} fusion(f32[1,16,64,128]{3,2,1,0:T(8,128)S(1)} %bitcast.78, f32[1,16,64,128]{3,2,1,0:T(8,128)S(1)} %bitcast.76, f32[15,64,128]{2,1,0:T(8,128)} %fusion.12), kind=kLoop, calls=%fused_computation.26 | loop fusion | flops 983040 | bytes 2523136 | tf_op jit(solution)/shard_map/mul | solution.py:145
  55.4 30.3 %all-reduce.2 = (f32[]{:T(128)}, f32[]{:T(128)}, f32[]{:T(128)}, f32[]{:T(128)}) all-reduce(f32[]{:T(128)} %get-tuple-element.3, f32[]{:T(128)} %get-tuple-element.4, f32[]{:T(128)} %get-tuple-element.5, f32[]{:T(128)} %get-tuple-element.2), channel_id=1, replica_groups=mesh['groups'=2,'gx'=4,'gy'=4] {'gx','gy'}, use_global_device_ids=true, to_apply=%region_5.0 | all-reduce | flops 4 | bytes 32 | tf_op jit(solution)/shard_map/psum | solution.py:59
  88.9 3.0 %copy.162 = f32[65,64,1]{2,0,1:T(8,128)} copy(f32[65,64,1]{0,1,2:T(8,128)} %collective-permute-done) | data formatting | bytes 33280 | tf_op jit(solution)/shard_map/ppermute | solution.py:20
  91.9 3.0 %copy.163 = f32[65,64,1]{2,0,1:T(8,128)} copy(f32[65,64,1]{0,1,2:T(8,128)} %collective-permute-done.1) | data formatting | bytes 33280 | tf_op jit(solution)/shard_map/ppermute | solution.py:22
  94.9 1.5 %pad_maximum_fusion.8 = f32[1,64,130]{2,0,1:T(1,128)S(1)} fusion(f32[65,64,1]{2,0,1:T(8,128)} %copy.163, f32[65,64,128]{2,0,1:T(8,128)S(1)} %dynamic-update-slice.4, f32[65,64,1]{2,0,1:T(8,128)} %copy.162), kind=kLoop, calls=%fused_computation.48 | loop fusion | flops 16640 | bytes 2196480 | tf_op jit(solution)/shard_map/slice | solution.py:101
  97.5 0.9 pad_maximum_fusion
  99.2 1.2 %copy.167 = f32[32,64,130]{2,1,0:T(8,128)S(1)} copy(f32[32,64,130]{2,0,1:T(8,128)S(1)} %pad_maximum_fusion) | data formatting | bytes 2129920 | tf_op jit(solution)/shard_map/slice | solution.py:40
  101.8 1.1 subtract_multiply_fusion
  106.6 0.9 pad_maximum_fusion.4
  (85 shorter events, 20.0 us)
Async XLA Ops:
  0.6 2.3 %copy-start.8 = (f32[2,16,64,128]{3,2,1,0:T(8,128)S(1)}, f32[2,16,64,128]{3,2,1,0:T(8,128)}, u32[]{:S(2)}) copy-start(f32[2,16,64,128]{3,2,1,0:T(8,128)} %param.10) | copy-start | bytes 3145732
  0.6 2.4 %copy-start.2 = (f32[16,64,128]{2,1,0:T(8,128)S(1)}, f32[16,64,128]{2,1,0:T(8,128)}, u32[]{:S(2)}) copy-start(f32[16,64,128]{2,1,0:T(8,128)} %param.9) | copy-start | bytes 1572868
  3.0 1.8 %copy-start.5 = (f32[1,16,64,128]{3,2,1,0:T(8,128)}, f32[1,16,64,128]{3,2,1,0:T(8,128)S(1)}, u32[]{:S(2)}) copy-start(f32[1,16,64,128]{3,2,1,0:T(8,128)S(1)} %get-tuple-element.19) | copy-start | bytes 1572868
  3.0 1.8 %copy-start.11 = (s32[64,128]{1,0:T(8,128)S(1)}, s32[64,128]{1,0:T(8,128)}, u32[]{:S(2)}) copy-start(s32[64,128]{1,0:T(8,128)} %param.11) | copy-start | bytes 98308
  3.0 1.8 %copy-start.13 = (s32[64,128]{1,0:T(8,128)S(1)}, s32[64,128]{1,0:T(8,128)}, u32[]{:S(2)}) copy-start(s32[64,128]{1,0:T(8,128)} %param.12) | copy-start | bytes 98308
  11.0 15.1 %copy-start.14 = (s32[128]{0:T(128)S(1)}, s32[128]{0:T(128)}, u32[]{:S(2)}) copy-start(s32[128]{0:T(128)} %param.15) | copy-start | bytes 1540
  11.0 16.3 %copy-start.3 = (f32[16,64,128]{2,1,0:T(8,128)S(1)}, f32[16,64,128]{2,1,0:T(8,128)}, u32[]{:S(2)}) copy-start(f32[16,64,128]{2,1,0:T(8,128)} %param.8) | copy-start | bytes 1572868
  11.0 77.9 %collective-permute-start = (f32[65,64,1]{0,1,2:T(8,128)}, f32[65,64,1]{0,1,2:T(8,128)}, u32[]{:S(2)}, u32[]{:S(2)}) collective-permute-start(f32[65,64,1]{0,1,2:T(8,128)} %copy.160), channel_id=1, source_target_pairs={{0,4},{4,8},{8,12},{12,0},{1,5},{5,9},{9,13},{13,1},{2,6},{6,10},{... | collective-permute-start | bytes 49928 | tf_op jit(solution)/shard_map/ppermute | solution.py:20
  17.1 74.8 %collective-permute-start.1 = (f32[65,64,1]{0,1,2:T(8,128)}, f32[65,64,1]{0,1,2:T(8,128)}, u32[]{:S(2)}, u32[]{:S(2)}) collective-permute-start(f32[65,64,1]{0,1,2:T(8,128)} %copy.161), channel_id=1, source_target_pairs={{4,0},{8,4},{12,8},{0,12},{5,1},{9,5},{13,9},{1,13},{6,2},{10,6},{... | collective-permute-start | bytes 49928 | tf_op jit(solution)/shard_map/ppermute | solution.py:22
  19.8 83.1 %collective-permute-start.2 = (f32[65,1,128]{2,0,1:T(8,128)}, f32[65,1,128]{2,0,1:T(8,128)}, u32[]{:S(2)}, u32[]{:S(2)}) collective-permute-start(f32[65,1,128]{2,0,1:T(8,128)} %get-tuple-element.17), channel_id=1, source_target_pairs={{1,0},{2,1},{3,2},{5,4},{6,5},{7,6},{9,8},{10,9},{11,10},{13,12},{... | collective-permute-start | bytes 99848 | tf_op jit(solution)/shard_map/ppermute | solution.py:22
  21.1 83.2 %collective-permute-start.3 = (f32[65,1,128]{2,0,1:T(8,128)}, f32[65,1,128]{2,0,1:T(8,128)}, u32[]{:S(2)}, u32[]{:S(2)}) collective-permute-start(f32[65,1,128]{2,0,1:T(8,128)} %get-tuple-element.16), channel_id=1, source_target_pairs={{0,1},{1,2},{2,3},{4,5},{5,6},{6,7},{8,9},{9,10},{10,11},{12,13},{... | collective-permute-start | bytes 99848 | tf_op jit(solution)/shard_map/ppermute | solution.py:20
  26.1 3.8 %copy-start.9 = (f32[1,16,64,128]{3,1,2,0:T(8,128)}, f32[1,16,64,128]{3,1,2,0:T(8,128)S(1)}, u32[]{:S(2)}) copy-start(f32[1,16,64,128]{3,1,2,0:T(8,128)S(1)} %copy.203) | copy-start | bytes 1572868
  47.7 7.0 %copy-start.10 = (f32[64,128]{1,0:T(8,128)S(1)}, f32[64,128]{1,0:T(8,128)}, u32[]{:S(2)}) copy-start(f32[64,128]{1,0:T(8,128)} %param.14) | copy-start | bytes 98308
  94.9 1.8 %copy-start = (f32[65,64,1]{2,0,1:T(8,128)S(1)}, f32[65,64,1]{2,0,1:T(8,128)}, u32[]{:S(2)}) copy-start(f32[65,64,1]{2,0,1:T(8,128)} %copy.162) | copy-start | bytes 49924
  94.9 2.5 %copy-start.1 = (f32[65,64,1]{2,0,1:T(8,128)S(1)}, f32[65,64,1]{2,0,1:T(8,128)}, u32[]{:S(2)}) copy-start(f32[65,64,1]{2,0,1:T(8,128)} %copy.163) | copy-start | bytes 49924
  101.8 2.5 %slice-start = ((f32[49,128]{1,0:T(8,128)}), f32[32,128]{1,0:T(8,128)S(1)}, s32[]{:S(2)}) async-start(f32[49,128]{1,0:T(8,128)} %select_bitcast_fusion), calls=%async_computation | async-start | bytes 32768 | tf_op jit(solution)/shard_map/slice | solution.py:84
  101.8 2.5 %slice-start.1 = ((f32[49,128]{1,0:T(8,128)}), f32[1,128]{1,0:T(1,128)S(1)}, s32[]{:S(2)}) async-start(f32[49,128]{1,0:T(8,128)} %select_bitcast_fusion), calls=%async_computation.1 | async-start | bytes 1024 | tf_op jit(solution)/shard_map/slice | solution.py:84
  104.3 1.1 copy-start.12
  106.4 1.2 %copy-start.6 = (f32[32,64,128]{2,1,0:T(8,128)S(1)}, f32[32,64,128]{2,1,0:T(8,128)}, u32[]{:S(2)}) copy-start(f32[32,64,128]{2,1,0:T(8,128)} %pad_maximum_fusion.6) | copy-start | bytes 3145732
  106.4 1.2 %slice-start.2 = ((f32[33,128]{1,0:T(8,128)}), f32[32,128]{1,0:T(8,128)S(1)}, s32[]{:S(2)}) async-start(f32[33,128]{1,0:T(8,128)} %copy-done.12), calls=%async_computation.2 | async-start | bytes 32768 | tf_op jit(solution)/shard_map/slice | solution.py:114
  107.6 1.0 copy-start.4
  107.6 1.4 %copy-start.7 = (f32[2,15,64,128]{3,2,1,0:T(8,128)S(1)}, f32[2,15,64,128]{3,2,1,0:T(8,128)}, u32[]{:S(2)}) copy-start(f32[2,15,64,128]{3,2,1,0:T(8,128)} %fusion.7) | copy-start | bytes 2949124
where the time goes:
time: 112 us; the launch traced here: 111 us
  blocking collectives  43.6 us (39%)
  local copies, waits for them, and re-layouts  32.9 us (29%)
  other arithmetic  20.6 us (18%)
  starting transfers between devices  10.1 us (9%)
  between operations  4.18 us (4%)
    psum x1, blocking collectives, shards(): lax.psum((jnp.sum(wet_area), jnp.sum(wet_area * rainfall_input), jnp.sum(...  30.3 us
    all_gather x1, blocking collectives, shards(): gathered = lax.all_gather(top_row, 'gx', axis=1, tiled=True)  13.3 us
    unnamed x37, local copies, waits for them, and re-layouts  7.21 us
    ppermute x2, starting transfers between devices, with_halo(): lax.ppermute(tail, axis, [(i, (i + 1) % count) for i in range(ends)])  6.7 us
    slice x3, local copies, waits for them, and re-layouts, with_halo(): lax.slice_in_dim(cells, cells.shape[dim] - width, cells.shape[dim], axis=...  6.57 us
    mul x2, other arithmetic, shards(): wet_cells[:-1] * wet_cells[1:] * vertical_mixing  4.14 us
    ppermute x2, starting transfers between devices, with_halo(): lax.ppermute(head, axis, [((i + 1) % count, i) for i in range(ends)])  3.37 us
    slice x1, local copies, waits for them, and re-layouts, with_halo(): head = lax.slice_in_dim(cells, 0, width, axis=dim)  3.07 us
  transfers between devices with their start and end apart: 4, of which 0 were waited for; matrix products, arithmetic and copies ran while one was open for 32% of the time, Pallas kernels for 0%

commit v1 on v0

--- a/solution.py
+++ b/solution.py
@@ -7,6 +7,10 @@
 diffusivity = 0.5
 vertical_mixing = 0.3
 top_thickness = 0.5
+
+
+def see_sides_over_axis(my_data, mesh_name):
+    return jnp.concatenate(lax.all_gather(my_data, axis_name=mesh_name), 1)
 
 
 def with_halo(cells, sides, width, closed):
@@ -78,7 +82,7 @@
         ],
         axis=0,
     )
-    gathered = lax.all_gather(top_row, "gx", axis=1, tiled=True)
+    gathered = see_sides_over_axis(top_row, "gx")
     partner_row = jnp.take(gathered, seam_partner_index, axis=1)
     partner_fields = jnp.concatenate(
         [partner_row[: 2 * layer_stack_number], partner_row[3 * layer_stack_number :]], axis=0

time: 112 us -> 106 us (0.946)
  local copies, waits for them, and re-layouts: 32.9 us -> 26.9 us
  blocking collectives: 43.6 us -> 45.9 us
  starting transfers between devices: 10.1 us -> 8.69 us
    ppermute x2, starting transfers between devices: 6.7 us -> 2.99 us  [with_halo(): lax.ppermute(tail, axis, [(i, (i + 1) % count) for i in range(ends)])]
    unnamed x37 -> x38, local copies, waits for them, and re-layouts: 7.21 us -> 4.14 us
    ppermute x2, starting transfers between devices: 3.37 us -> 5.7 us  [with_halo(): lax.ppermute(head, axis, [((i + 1) % count, i) for i in range(ends)])]
    psum x1, blocking collectives: 30.3 us -> 32.4 us  [shards(): lax.psum((jnp.sum(wet_area), jnp.sum(wet_area * rainfall_input), jnp.sum(...]
    concatenate x2, other arithmetic: 1.83 us -> 3.49 us  [with_halo(): jnp.concatenate([lax.ppermute(tail, axis, [(i, (i + 1) % count) for i in...]
    gather x2, local copies, waits for them, and re-layouts: 2.28 us -> 0.72 us  [shards(): partner_row = jnp.take(gathered, seam_partner_index, axis=1)]
    slice x2 -> x1, other arithmetic: 2.16 us -> 0.74 us  [shards(): north_speed[:, :-1, :]]
    slice x1 -> x2, local copies, waits for them, and re-layouts: 3.07 us -> 4.04 us  [with_halo(): head = lax.slice_in_dim(cells, 0, width, axis=dim)]
  transfers between devices with their start and end apart: 4 -> 4, of which waited for: 0 -> 0; matrix products, arithmetic and copies ran while one was open for 32% -> 34% of each run, Pallas kernels for 0% -> 0%
where the time goes in v1:
time: 106 us; the launch traced here: 105 us
  blocking collectives  45.9 us (43%)
  local copies, waits for them, and re-layouts  26.9 us (25%)
  other arithmetic  19.7 us (19%)
  starting transfers between devices  8.69 us (8%)
  between operations  4.33 us (4%)
    psum x1, blocking collectives, shards(): lax.psum((jnp.sum(wet_area), jnp.sum(wet_area * rainfall_input), jnp.sum(...  32.4 us
    all_gather x1, blocking collectives, see_sides_over_axis(): return jnp.concatenate(lax.all_gather(my_data, axis_name=mesh_name), 1)  13.5 us
    slice x2, local copies, waits for them, and re-layouts, with_halo(): lax.slice_in_dim(cells, cells.shape[dim] - width, cells.shape[dim], axis=...  6.18 us
    ppermute x2, starting transfers between devices, with_halo(): lax.ppermute(head, axis, [((i + 1) % count, i) for i in range(ends)])  5.7 us
    mul x2, other arithmetic, shards(): wet_cells[:-1] * wet_cells[1:] * vertical_mixing  4.18 us
    unnamed x38, local copies, waits for them, and re-layouts  4.14 us
    slice x2, local copies, waits for them, and re-layouts, with_halo(): head = lax.slice_in_dim(cells, 0, width, axis=dim)  4.04 us
    ppermute x1, local copies, waits for them, and re-layouts, with_halo(): lax.ppermute(head, axis, [((i + 1) % count, i) for i in range(ends)])  3.78 us
  transfers between devices with their start and end apart: 4, of which 0 were waited for; matrix products, arithmetic and copies ran while one was open for 34% of the time, Pallas kernels for 0%

profile of v1, /device:TPU:0, one launch (start us, length us, event | category | flops | bytes accessed | tf_op | source)
XLA Modules:
  0.0 105.5 jit_solution(128760723017248713)
XLA Ops:
  0.7 1.2 %constant_dynamic-update-slice_fusion.2 = f32[65,64,128]{2,1,0:T(8,128)S(1)} fusion(f32[16,64,128]{2,1,0:T(8,128)} %param.8), kind=kLoop, calls=%fused_computation.71 | loop fusion | bytes 1048576
  1.8 1.1 %constant_dynamic-update-slice_fusion.1 = f32[65,64,128]{2,1,0:T(8,128)S(1)} fusion(f32[65,64,128]{2,1,0:T(8,128)S(1)} %constant_dynamic-update-slice_fusion.2, f32[16,64,128]{2,1,0:T(8,128)} %param.9), kind=kLoop, calls=%fused_computation.70 | loop fusion | bytes 1048576
  3.8 3.0 %collective-permute-start.3 = (f32[65,1,128]{2,1,0:T(1,128)}, f32[65,1,128]{2,1,0:T(1,128)}, u32[]{:S(2)}, u32[]{:S(2)}) collective-permute-start(f32[65,1,128]{2,1,0:T(1,128)} %get-tuple-element.17), channel_id=1, source_target_pairs={{0,1},{1,2},{2,3},{4,5},{5,6},{6,7},{8,9},{9,10},{10,11},{12,13},{... | collective-permute-start | bytes 99848 | tf_op jit(solution)/shard_map/ppermute | solution.py:24
  6.7 1.3 %collective-permute-start.2 = (f32[65,1,128]{2,1,0:T(1,128)}, f32[65,1,128]{2,1,0:T(1,128)}, u32[]{:S(2)}, u32[]{:S(2)}) collective-permute-start(f32[65,1,128]{2,1,0:T(1,128)} %get-tuple-element.16), channel_id=1, source_target_pairs={{1,0},{2,1},{3,2},{5,4},{6,5},{7,6},{9,8},{10,9},{11,10},{13,12},{... | collective-permute-start | bytes 99848 | tf_op jit(solution)/shard_map/ppermute | solution.py:26
  8.0 2.8 %fusion.23 = (f32[65,64,1]{2,1,0:T(8,128)}, f32[65,64,1]{2,1,0:T(8,128)}) fusion(f32[65,64,128]{2,1,0:T(8,128)S(1)} %get-tuple-element.12), kind=kLoop, calls=%fused_computation.80 | loop fusion | bytes 66560 | tf_op jit(solution)/shard_map/slice | solution.py:21
  10.9 3.4 %copy.92 = f32[65,64,1]{0,1,2:T(8,128)} copy(f32[65,64,1]{2,1,0:T(8,128)} %get-tuple-element.15) | data formatting | bytes 33280 | tf_op jit(solution)/shard_map/slice | solution.py:20
  14.2 4.4 %collective-permute-start.1 = (f32[65,64,1]{0,1,2:T(8,128)}, f32[65,64,1]{0,1,2:T(8,128)}, u32[]{:S(2)}, u32[]{:S(2)}) collective-permute-start(f32[65,64,1]{0,1,2:T(8,128)} %copy.92), channel_id=1, source_target_pairs={{4,0},{8,4},{12,8},{0,12},{5,1},{9,5},{13,9},{1,13},{6,2},{10,6},{... | collective-permute-start | bytes 49928 | tf_op jit(solution)/shard_map/ppermute | solution.py:26
  18.7 3.3 %copy.91 = f32[65,64,1]{0,1,2:T(8,128)} copy(f32[65,64,1]{2,1,0:T(8,128)} %get-tuple-element.14) | data formatting | bytes 33280 | tf_op jit(solution)/shard_map/slice | solution.py:21
  22.0 1.1 %slice_bitcast_fusion.1 = f32[16,64,128]{2,1,0:T(8,128)S(1)} fusion(f32[2,16,64,128]{3,2,1,0:T(8,128)} %param.10), kind=kLoop, calls=%fused_computation.38 | loop fusion | bytes 1048576 | tf_op jit(solution)/shard_map/squeeze | solution.py:97
  24.3 1.1 %pad_maximum_fusion.6 = f32[32,64,128]{2,1,0:T(8,128)} fusion(f32[16,64,128]{2,1,0:T(8,128)S(1)} %copy-done.2, f32[16,64,128]{2,1,0:T(8,128)S(1)} %copy-done.3), kind=kLoop, calls=%fused_computation.21 | loop fusion | flops 262144 | bytes 2097152 | tf_op jit(solution)/shard_map/concatenate | solution.py:92
  25.4 0.8 fusion.9
  26.2 13.5 %all-gather.1 = f32[4,49,128]{2,1,0:T(8,128)S(1)} all-gather(f32[1,49,128]{2,1,0:T(8,128)S(1)} %maximum_bitcast_fusion.2), channel_id=2, replica_groups=mesh['groups'=2,'gx'=4,'gy'=4] {'gx'}, dimensions={0}, use_global_device_ids=true | all-gather | bytes 125440 | tf_op jit(solution)/shard_map/all_gather | solution.py:13
  41.3 2.1 %fusion.10 = f32[15,64,128]{2,1,0:T(8,128)} fusion(f32[16,64,128]{2,1,0:T(8,128)} %fusion.9), kind=kLoop, calls=%fused_computation.43 | loop fusion | flops 245760 | bytes 1474560 | tf_op jit(solution)/shard_map/mul | solution.py:149
  43.4 0.8 convert_multiply_fusion
  45.5 2.1 %fusion.7 = f32[2,15,64,128]{3,2,1,0:T(8,128)} fusion(f32[1,16,64,128]{3,2,1,0:T(8,128)S(1)} %bitcast.74, f32[1,16,64,128]{3,2,1,0:T(8,128)S(1)} %bitcast.72, f32[15,64,128]{2,1,0:T(8,128)} %fusion.10), kind=kLoop, calls=%fused_computation.26 | loop fusion | flops 983040 | bytes 2523136 | tf_op jit(solution)/shard_map/mul | solution.py:149
  48.4 32.4 %all-reduce.2 = (f32[]{:T(128)}, f32[]{:T(128)}, f32[]{:T(128)}, f32[]{:T(128)}) all-reduce(f32[]{:T(128)} %get-tuple-element.3, f32[]{:T(128)} %get-tuple-element.4, f32[]{:T(128)} %get-tuple-element.5, f32[]{:T(128)} %get-tuple-element.2), channel_id=1, replica_groups=mesh['groups'=2,'gx'=4,'gy'=4] {'gx','gy'}, use_global_device_ids=true, to_apply=%region_5.0 | all-reduce | flops 4 | bytes 32 | tf_op jit(solution)/shard_map/psum | solution.py:63
  84.0 3.8 %copy.94 = f32[65,64,1]{2,1,0:T(8,128)} copy(f32[65,64,1]{0,1,2:T(8,128)} %collective-permute-done.1) | data formatting | bytes 33280 | tf_op jit(solution)/shard_map/ppermute | solution.py:26
  87.8 3.7 %copy.93 = f32[65,64,1]{2,1,0:T(8,128)} copy(f32[65,64,1]{0,1,2:T(8,128)} %collective-permute-done) | data formatting | bytes 33280 | tf_op jit(solution)/shard_map/ppermute | solution.py:24
  91.5 2.6 %pad_maximum_fusion = f32[32,64,130]{2,1,0:T(8,128)S(1)} fusion(f32[65,64,1]{2,1,0:T(8,128)} %copy.94, f32[65,64,128]{2,1,0:T(8,128)S(1)} %get-tuple-element.12, f32[65,64,1]{2,1,0:T(8,128)} %copy.93), kind=kLoop, calls=%fused_computation.1 | loop fusion | flops 532480 | bytes 3228160 | tf_op jit(solution)/shard_map/concatenate | solution.py:22
  95.4 1.1 %subtract_multiply_fusion = f32[2,16,64,129]{3,2,1,0:T(8,128)S(1)} fusion(f32[2,16,64,130]{3,2,1,0:T(8,128)S(1)} %bitcast.71, f32[16,64,129]{2,1,0:T(8,128)S(1)} %get-tuple-element.23, f32[16,64,129]{2,1,0:T(8,128)S(1)} %get-tuple-element.10, f32[16,64,129]{2,1,0:T(8,128)S(1)} %get-tuple-element.22), kind=kLoop, calls=%fused_computation.3 | loop fusion | flops 1849344 | bytes 4755456 | tf_op jit(solution)/shard_map/mul | solution.py:35
  100.6 0.9 pad_maximum_fusion.3
  102.0 0.8 copy-done.4
  103.7 0.8 slice_bitcast_fusion
  104.6 0.8 pad_maximum_fusion.9
  (84 shorter events, 12.3 us)
Async XLA Ops:
  0.6 2.3 %copy-start.7 = (f32[2,16,64,128]{3,2,1,0:T(8,128)S(1)}, f32[2,16,64,128]{3,2,1,0:T(8,128)}, u32[]{:S(2)}) copy-start(f32[2,16,64,128]{3,2,1,0:T(8,128)} %param.10) | copy-start | bytes 3145732
  0.6 2.4 %copy-start.11 = (s32[64,128]{1,0:T(8,128)S(1)}, s32[64,128]{1,0:T(8,128)}, u32[]{:S(2)}) copy-start(s32[64,128]{1,0:T(8,128)} %param.11) | copy-start | bytes 98308
  0.7 2.4 %copy-start.15 = (s32[64,128]{1,0:T(8,128)S(1)}, s32[64,128]{1,0:T(8,128)}, u32[]{:S(2)}) copy-start(s32[64,128]{1,0:T(8,128)} %param.12) | copy-start | bytes 98308
  3.1 22.3 %copy-start.8 = (f32[64,128]{1,0:T(8,128)}, f32[64,128]{1,0:T(8,128)S(1)}, u32[]{:S(2)}) copy-start(f32[64,128]{1,0:T(8,128)S(1)} %get-tuple-element.13) | copy-start | bytes 98308
  3.8 94.1 %collective-permute-start.3 = (f32[65,1,128]{2,1,0:T(1,128)}, f32[65,1,128]{2,1,0:T(1,128)}, u32[]{:S(2)}, u32[]{:S(2)}) collective-permute-start(f32[65,1,128]{2,1,0:T(1,128)} %get-tuple-element.17), channel_id=1, source_target_pairs={{0,1},{1,2},{2,3},{4,5},{5,6},{6,7},{8,9},{9,10},{10,11},{12,13},{... | collective-permute-start | bytes 99848 | tf_op jit(solution)/shard_map/ppermute | solution.py:24
  6.7 89.7 %collective-permute-start.2 = (f32[65,1,128]{2,1,0:T(1,128)}, f32[65,1,128]{2,1,0:T(1,128)}, u32[]{:S(2)}, u32[]{:S(2)}) collective-permute-start(f32[65,1,128]{2,1,0:T(1,128)} %get-tuple-element.16), channel_id=1, source_target_pairs={{1,0},{2,1},{3,2},{5,4},{6,5},{7,6},{9,8},{10,9},{11,10},{13,12},{... | collective-permute-start | bytes 99848 | tf_op jit(solution)/shard_map/ppermute | solution.py:26
  14.2 8.9 %copy-start.2 = (f32[16,64,128]{2,1,0:T(8,128)S(1)}, f32[16,64,128]{2,1,0:T(8,128)}, u32[]{:S(2)}) copy-start(f32[16,64,128]{2,1,0:T(8,128)} %param.9) | copy-start | bytes 1572868
  14.2 8.9 %copy-start.3 = (f32[16,64,128]{2,1,0:T(8,128)S(1)}, f32[16,64,128]{2,1,0:T(8,128)}, u32[]{:S(2)}) copy-start(f32[16,64,128]{2,1,0:T(8,128)} %param.8) | copy-start | bytes 1572868
  14.2 8.9 %copy-start.16 = (s32[128]{0:T(128)S(1)}, s32[128]{0:T(128)}, u32[]{:S(2)}) copy-start(s32[128]{0:T(128)} %param.15) | copy-start | bytes 1540
  14.2 69.8 %collective-permute-start.1 = (f32[65,64,1]{0,1,2:T(8,128)}, f32[65,64,1]{0,1,2:T(8,128)}, u32[]{:S(2)}, u32[]{:S(2)}) collective-permute-start(f32[65,64,1]{0,1,2:T(8,128)} %copy.92), channel_id=1, source_target_pairs={{4,0},{8,4},{12,8},{0,12},{5,1},{9,5},{13,9},{1,13},{6,2},{10,6},{... | collective-permute-start | bytes 49928 | tf_op jit(solution)/shard_map/ppermute | solution.py:26
  22.0 65.8 %collective-permute-start = (f32[65,64,1]{0,1,2:T(8,128)}, f32[65,64,1]{0,1,2:T(8,128)}, u32[]{:S(2)}, u32[]{:S(2)}) collective-permute-start(f32[65,64,1]{0,1,2:T(8,128)} %copy.91), channel_id=1, source_target_pairs={{0,4},{4,8},{8,12},{12,0},{1,5},{5,9},{9,13},{13,1},{2,6},{6,10},{... | collective-permute-start | bytes 49928 | tf_op jit(solution)/shard_map/ppermute | solution.py:24
  26.2 13.5 %copy-start.13 = (f32[16,1,128]{2,1,0:T(1,128)}, f32[16,1,128]{2,1,0:T(1,128)S(1)}, u32[]{:S(2)}) copy-start(f32[16,1,128]{2,1,0:T(1,128)S(1)} %slice.183) | copy-start | bytes 24580
  41.3 6.4 %copy-start.10 = (f32[64,128]{1,0:T(8,128)S(1)}, f32[64,128]{1,0:T(8,128)}, u32[]{:S(2)}) copy-start(f32[64,128]{1,0:T(8,128)} %param.14) | copy-start | bytes 98308
  44.8 43.0 %copy-start.12 = (f32[49,128]{1,0:T(8,128)}, f32[49,128]{1,0:T(8,128)S(1)}, u32[]{:S(2)}) copy-start(f32[49,128]{1,0:T(8,128)S(1)} %select_bitcast_fusion) | copy-start | bytes 75268
  91.5 2.6 %copy-start = (f32[65,64,1]{2,1,0:T(8,128)S(1)}, f32[65,64,1]{2,1,0:T(8,128)}, u32[]{:S(2)}) copy-start(f32[65,64,1]{2,1,0:T(8,128)} %copy.93) | copy-start | bytes 49924
  91.5 2.9 %copy-start.1 = (f32[65,64,1]{2,1,0:T(8,128)S(1)}, f32[65,64,1]{2,1,0:T(8,128)}, u32[]{:S(2)}) copy-start(f32[65,64,1]{2,1,0:T(8,128)} %copy.94) | copy-start | bytes 49924
  95.4 2.4 %slice-start = ((f32[49,128]{1,0:T(8,128)}), f32[1,128]{1,0:T(1,128)S(1)}, s32[]{:S(2)}) async-start(f32[49,128]{1,0:T(8,128)} %copy-done.12), calls=%async_computation | async-start | bytes 1024 | tf_op jit(solution)/shard_map/slice | solution.py:88
  95.4 2.4 %slice-start.1 = ((f32[49,128]{1,0:T(8,128)}), f32[32,128]{1,0:T(8,128)S(1)}, s32[]{:S(2)}) async-start(f32[49,128]{1,0:T(8,128)} %copy-done.12), calls=%async_computation.1 | async-start | bytes 32768 | tf_op jit(solution)/shard_map/slice | solution.py:88
  97.8 1.2 %copy-start.14 = (f32[33,128]{1,0:T(8,128)}, f32[33,128]{1,0:T(8,128)S(1)}, u32[]{:S(2)}) copy-start(f32[33,128]{1,0:T(8,128)S(1)} %maximum_select_fusion) | copy-start | bytes 50692
  98.9 0.8 copy-start.9
  100.4 1.2 %copy-start.5 = (f32[32,64,128]{2,1,0:T(8,128)S(1)}, f32[32,64,128]{2,1,0:T(8,128)}, u32[]{:S(2)}) copy-start(f32[32,64,128]{2,1,0:T(8,128)} %pad_maximum_fusion.6) | copy-start | bytes 3145732
  100.4 1.2 %slice-start.2 = ((f32[33,128]{1,0:T(8,128)}), f32[32,128]{1,0:T(8,128)S(1)}, s32[]{:S(2)}) async-start(f32[33,128]{1,0:T(8,128)} %copy-done.14), calls=%async_computation.2 | async-start | bytes 32768 | tf_op jit(solution)/shard_map/slice | solution.py:118
  101.7 1.0 copy-start.4
  101.7 1.4 %copy-start.6 = (f32[2,15,64,128]{3,2,1,0:T(8,128)S(1)}, f32[2,15,64,128]{3,2,1,0:T(8,128)}, u32[]{:S(2)}) copy-start(f32[2,15,64,128]{3,2,1,0:T(8,128)} %fusion.7) | copy-start | bytes 2949124
  (1 other events, 0.7 us)
